TPU v7x, 32 devices: a whole 2x2x4 slice. The times are simulated.
32 devices in a mesh: blk: 16 (over z, y, core), rel: 2 (over x).
Axes of the slice: x: 2, y: 2, z: 4, core: 2. Of those that a mesh axis runs over, the one named last changes fastest.
Arguments:
- source_table: float32 [400, 24576], P(None, ('blk', 'rel')), may hold values from -1.2 to 1.2
- source_state: float32 [24576], P(('blk', 'rel')), may hold values from 0.001 to 0.1
- target_table: float32 [400, 24576], P(None, ('blk', 'rel')), may hold values from -1.2 to 1.2
- target_state: float32 [24576], P(('blk', 'rel')), may hold values from 0.001 to 0.1
- relation_ops: float32 [400, 2048], P(None, 'blk'), may hold values from 0.5 to 1.5
- relation_state: float32 [400, 2048], P(None, 'blk'), may hold values from 0.01 to 1
- source_ids: int32 [2, 16384], P(None, ('blk', 'rel')), may hold values from 0 to 767
- target_ids: int32 [2, 16384], P(None, ('blk', 'rel')), may hold values from 0 to 767
- relation_ids: int32 [2, 16384], P(None, ('blk', 'rel')), may hold values from 0 to 127
- negative_ids: int32 [2, 16384], P(None, ('blk', 'rel')), may hold values from 0 to 767
Outputs:
- new_source: float32 [400, 24576], P(None, ('blk', 'rel'))
- new_source_state: float32 [24576], P(('blk', 'rel'))
- held_target: float32 [400, 24576], P(None, ('blk', 'rel'))
- held_target_state: float32 [24576], P(('blk', 'rel'))
- new_relations: float32 [400, 2048], P(None, 'blk')
- new_relation_state: float32 [400, 2048], P(None, 'blk')
All inputs are finite; a program needn't handle non-finite values.
Results may differ from a plain program's by a relative error of at most 0.0001.
Values sent between devices are 32-bit elements; how exact they have to be, the bound alone decides.
A program may use at most 64 MiB of HBM per device.

v0:
```python
import jax
import jax.numpy as jnp
from jax import lax
from jax.sharding import PartitionSpec as P

learn_rate = 0.1
epsilon = 1e-06
HIGHEST = lax.Precision.HIGHEST


def passed_along(value, axis, steps):
    count = lax.axis_size(axis)
    pairs = [(source, (source + steps) % count) for source in range(count)]
    return lax.ppermute(value, axis, pairs)


def one_hot(labels, length):
    return (
        lax.broadcasted_iota(jnp.int32, (length, labels.shape[0]), 0) == labels[None, :]
    ).astype(jnp.float32)


def pick_columns(matrix, selector):
    return jnp.dot(matrix, selector, precision=HIGHEST)


def add_columns(values, selector):
    return lax.dot_general(values, selector, (((1,), (1,)), ((), ())), precision=HIGHEST)


def row_adagrad(matrix, row_state, gradient):
    fresh = row_state + jnp.mean(gradient * gradient, axis=0)
    return (matrix - learn_rate * gradient / (jnp.sqrt(fresh) + epsilon)[None, :], fresh)


def bucket_terms(
    source_side, target_side, relations, source_idx, target_idx, relation_idx, negative_idx
):
    row_total = source_side.shape[1]
    edge_total = source_idx.shape[0]
    neg_total = negative_idx.shape[0]
    source_hot = one_hot(source_idx, row_total)
    target_hot = one_hot(jnp.concatenate([target_idx, negative_idx]), row_total)
    relation_hot = one_hot(relation_idx, relations.shape[1])
    source = pick_columns(source_side, source_hot)
    picked = pick_columns(target_side, target_hot)
    target = picked[:, :edge_total]
    negative = picked[:, edge_total:]
    relation = pick_columns(relations, relation_hot)
    queries = source * relation
    positive = jnp.sum(queries * target, axis=0)
    neg_score = lax.dot_general(queries, negative, (((0,), (0,)), ((), ())), precision=HIGHEST)
    pos_coef = -jax.nn.sigmoid(-positive)
    neg_coef = jax.nn.sigmoid(neg_score) / neg_total
    grad_query = target * pos_coef[None, :] + lax.dot_general(
        negative, neg_coef, (((1,), (1,)), ((), ())), precision=HIGHEST
    )
    grad_target = queries * pos_coef[None, :]
    grad_negative = jnp.dot(queries, neg_coef, precision=HIGHEST)
    target_grad = add_columns(jnp.concatenate([grad_target, grad_negative], axis=1), target_hot)
    relation_grad = add_columns(grad_query * source, relation_hot)
    return (target_grad, grad_query * relation, source_hot, relation_grad)


def per_device(
    source_table,
    source_state,
    target_table,
    target_state,
    relation_ops,
    relation_state,
    source_ids,
    target_ids,
    relation_ids,
    negative_ids,
):
    bucket_count = source_ids.shape[0]
    source_side, source_rows = (source_table, source_state)
    target_side, target_rows = (target_table, target_state)
    collected = []
    for bucket in range(bucket_count):
        target_grad, query_grad, source_hot, relation_grad = bucket_terms(
            source_side,
            target_side,
            relation_ops,
            source_ids[bucket],
            target_ids[bucket],
            relation_ids[bucket],
            negative_ids[bucket],
        )
        last = bucket + 1 >= bucket_count
        target_side, target_rows = row_adagrad(target_side, target_rows, target_grad)
        if not last:
            target_side, target_rows = passed_along((target_side, target_rows), "blk", 1)
        source_side, source_rows = row_adagrad(
            source_side, source_rows, add_columns(query_grad, source_hot)
        )
        collected.append(relation_grad)
    summed = collected[0]
    for extra_grad in collected[1:]:
        summed = summed + extra_grad
    summed = lax.psum(summed, "rel")
    new_relation_state = relation_state + summed * summed
    new_relations = relation_ops - learn_rate * summed / (jnp.sqrt(new_relation_state) + epsilon)
    return (source_side, source_rows, target_side, target_rows, new_relations, new_relation_state)


def solution(mesh):
    placed = (
        P(None, ("blk", "rel")),
        P(("blk", "rel")),
        P(None, ("blk", "rel")),
        P(("blk", "rel")),
        P(None, "blk"),
        P(None, "blk"),
        P(None, ("blk", "rel")),
        P(None, ("blk", "rel")),
        P(None, ("blk", "rel")),
        P(None, ("blk", "rel")),
    )
    return jax.shard_map(
        per_device,
        mesh=mesh,
        in_specs=placed,
        out_specs=(
            P(None, ("blk", "rel")),
            P(("blk", "rel")),
            P(None, ("blk", "rel")),
            P(("blk", "rel")),
            P(None, "blk"),
            P(None, "blk"),
        ),
        check_vma=False,
    )
```

profile of v0, /device:TPU:0, one launch (start us, length us, event | category | flops | bytes accessed | tf_op | source)
XLA Modules:
  0.0 87.9 jit_solution(15524736125075517416)
XLA Ops:
  7.2 0.0 all-reduce.2.cloned.1.call-start
  7.2 0.8 fusion.51
  8.0 0.8 fusion.52
  8.7 0.8 fusion.50
  9.5 0.8 fusion.53
  10.3 1.4 %convolution_bitcast_fusion.1 = f32[400,512]{1,0:T(8,128)S(1)} fusion(f32[400,128]{1,0:T(8,128)} %param.14, s32[512]{0:T(512)S(1)} %bitcast.33), kind=kOutput, calls=%fused_computation.36 | convolution fusion | flops 314638336 | bytes 1026048 | tf_op jit(solution)/shard_map/dot_general | solution.py:24
  11.7 0.0 copy-start
  11.7 3.6 %fusion.18 = f32[400,1024]{1,0:T(8,128)S(1)} fusion(f32[400,768]{1,0:T(8,128)} %param.12, s32[1024]{0:T(1024)S(1)} %pad_add_fusion), kind=kOutput, calls=%fused_computation.22 | convolution fusion | flops 3775660032 | bytes 2871296 | tf_op jit(solution)/shard_map/dot_general | solution.py:24
  15.4 0.0 copy-done
  15.4 1.3 %multiply_reduce_fusion.5 = (f32[512]{0:T(512)S(1)}, f32[400,512]{1,0:T(8,128)S(1)}, f32[400,512]{1,0:T(8,128)S(1)}) fusion(f32[400,1024]{1,0:T(8,128)S(1)} %fusion.18, f32[400,512]{1,0:T(8,128)S(1)} %convolution_bitcast_fusion.1, f32[400,768]{1,0:T(8,128)S(1)} %copy-done, s32[512]{0:T(512)S(1)} %bitcast.29), kind=kOutput, calls=%fused_computation.53 | convolution fusion | flops 1888443904 | bytes 4509696 | tf_op jit(solution)/shard_map/dot_general | solution.py:24
  16.7 2.1 %fusion.26 = f32[512,512]{1,0:T(8,128)S(1)} fusion(f32[400,512]{1,0:T(8,128)S(1)} %get-tuple-element.17, f32[400,1024]{1,0:T(8,128)S(1)} %fusion.18), kind=kOutput, calls=%fused_computation.32 | convolution fusion | flops 1259339776 | bytes 2686976 | tf_op jit(solution)/shard_map/dot_general | solution.py:52
  18.8 0.1 broadcast_multiply_fusion.1
  18.9 1.5 %fusion.54 = f32[400,512]{1,0:T(8,128)S(1)} fusion(f32[400,512]{1,0:T(8,128)S(1)} %get-tuple-element.17, f32[512,512]{1,0:T(8,128)S(1)} %fusion.26), kind=kOutput, calls=%fused_computation.91 | convolution fusion | flops 1258291200 | bytes 2686976 | tf_op jit(solution)/shard_map/dot_general | solution.py:59
  20.4 0.0 copy-start.8
  20.4 0.0 copy-start.2
  20.4 2.4 %multiply_reduce_fusion.2 = (f32[768]{0:T(1024)S(1)}, f32[400,768]{1,0:T(8,128)S(1)}) fusion(s32[1024]{0:T(1024)S(1)} %pad_add_fusion, f32[400,512]{1,0:T(8,128)S(1)} %fusion.54, f32[400,512]{1,0:T(8,128)S(1)} %broadcast_multiply_fusion.1), kind=kOutput, calls=%fused_computation.42 | convolution fusion | flops 3776683264 | bytes 2874368 | tf_op jit(solution)/shard_map/dot_general | solution.py:28
  22.8 0.0 copy-done.8
  22.9 0.6 collective-permute-start.1
  23.4 0.0 copy-done.2
  23.4 0.2 divide_subtract_fusion.2
  23.6 2.9 %collective-permute-start = (f32[400,768]{1,0:T(8,128)S(1)}, f32[400,768]{1,0:T(8,128)S(1)}, u32[]{:S(2)}, u32[]{:S(2)}) collective-permute-start(f32[400,768]{1,0:T(8,128)S(1)} %divide_subtract_fusion.2), channel_id=1, source_target_pairs={{0,2},{2,4},{4,6},{6,8},{8,10},{10,12},{12,14},{14,16},{16,18},{18... | collective-permute-start | bytes 3686408 | tf_op jit(solution)/shard_map/ppermute | solution.py:14
  26.4 1.5 %convolution_add_fusion = f32[400,512]{1,0:T(8,128)S(1)} fusion(f32[512,512]{1,0:T(8,128)S(1)} %fusion.26, f32[400,1024]{1,0:T(8,128)S(1)} %fusion.18, f32[512]{0:T(512)S(1)} %divide_negate_fusion.1), kind=kOutput, calls=%fused_computation.34 | convolution fusion | flops 1258700800 | bytes 3508224 | tf_op jit(solution)/shard_map/dot_general | solution.py:55
  28.0 0.0 copy-start.7
  28.0 0.0 copy-start.1
  28.0 1.4 %multiply_reduce_fusion.3 = (f32[768]{0:T(1024)S(1)}, f32[400,768]{1,0:T(8,128)S(1)}) fusion(s32[512]{0:T(512)S(1)} %bitcast.30, f32[400,512]{1,0:T(8,128)S(1)} %convolution_add_fusion, f32[400,512]{1,0:T(8,128)S(1)} %convolution_bitcast_fusion.1), kind=kOutput, calls=%fused_computation.44 | convolution fusion | flops 1888648448 | bytes 2872320 | tf_op jit(solution)/shard_map/dot_general | solution.py:28
  29.4 0.0 copy-done.7
  29.4 0.0 copy-done.1
  29.4 0.5 convolution_bitcast_fusion
  29.9 0.6 fusion.29
  30.5 12.8 %collective-permute-done = f32[400,768]{1,0:T(8,128)S(1)} collective-permute-done((f32[400,768]{1,0:T(8,128)S(1)}, f32[400,768]{1,0:T(8,128)S(1)}, u32[]{:S(2)}, u32[]{:S(2)}) %collective-permute-start) | collective-permute-done | bytes 1228832 | tf_op jit(solution)/shard_map/ppermute | solution.py:14
  43.2 0.0 copy-start.3
  43.2 2.3 %fusion.1 = f32[400,1024]{1,0:T(8,128)S(1)} fusion(f32[400,768]{1,0:T(8,128)S(1)} %collective-permute-done, s32[1024]{0:T(1024)S(1)} %pad_add_fusion.1), kind=kOutput, calls=%fused_computation.2 | convolution fusion | flops 3775660032 | bytes 2871296 | tf_op jit(solution)/shard_map/dot_general | solution.py:24
  45.6 0.0 copy-done.3
  45.6 1.4 %multiply_reduce_fusion.4 = (f32[512]{0:T(512)S(1)}, f32[400,512]{1,0:T(8,128)S(1)}, f32[400,512]{1,0:T(8,128)S(1)}) fusion(f32[400,1024]{1,0:T(8,128)S(1)} %fusion.1, f32[400,512]{1,0:T(8,128)S(1)} %convolution_bitcast_fusion, s32[512]{0:T(512)S(1)} %bitcast.35, f32[400,768]{1,0:T(8,128)S(1)} %copy-done, f32[400,768]{1,0:T(8,128)S(1)} %get-tuple-element.30, ...), kind=kOutput, calls=%fused_computation.51 | convolution fusion | flops 1889365504 | bytes 5741568 | tf_op jit(solution)/shard_map/dot_general | solution.py:24
  47.0 2.1 %fusion.22 = f32[512,512]{1,0:T(8,128)S(1)} fusion(f32[400,512]{1,0:T(8,128)S(1)} %get-tuple-element.13, f32[400,1024]{1,0:T(8,128)S(1)} %fusion.1), kind=kOutput, calls=%fused_computation.27 | convolution fusion | flops 1259339776 | bytes 2686976 | tf_op jit(solution)/shard_map/dot_general | solution.py:52
  49.1 0.1 broadcast_multiply_fusion
  49.2 1.5 %multiply_add_fusion = f32[400,512]{1,0:T(8,128)S(1)} fusion(f32[512,512]{1,0:T(8,128)S(1)} %fusion.22, f32[400,1024]{1,0:T(8,128)S(1)} %fusion.1, f32[512]{0:T(512)S(1)} %divide_negate_fusion), kind=kOutput, calls=%fused_computation.50 | convolution fusion | flops 1258700800 | bytes 3508224 | tf_op jit(solution)/shard_map/dot_general | solution.py:55
  50.7 2.4 %fusion.55 = f32[400,512]{1,0:T(8,128)} fusion(f32[400,512]{1,0:T(8,128)S(1)} %get-tuple-element.13, f32[512,512]{1,0:T(8,128)S(1)} %fusion.22), kind=kOutput, calls=%fused_computation.92 | convolution fusion | flops 1258291200 | bytes 2686976 | tf_op jit(solution)/shard_map/dot_general | solution.py:59
  53.1 2.6 %multiply_reduce_fusion.1 = (f32[768]{0:T(1024)S(1)}, f32[400,768]{1,0:T(8,128)}) fusion(s32[512]{0:T(512)S(1)} %bitcast.36, f32[400,512]{1,0:T(8,128)S(1)} %multiply_add_fusion, f32[400,512]{1,0:T(8,128)S(1)} %convolution_bitcast_fusion), kind=kOutput, calls=%fused_computation.40 | convolution fusion | flops 1888648448 | bytes 2872320 | tf_op jit(solution)/shard_map/dot_general | solution.py:28
  55.7 0.6 sqrt_add_fusion.1
  56.3 1.2 %convolution_add_fusion.1 = f32[400,128]{1,0:T(8,128)} fusion(f32[400,128]{1,0:T(8,128)S(1)} %fusion.29, f32[400,512]{1,0:T(8,128)S(1)} %multiply_add_fusion, f32[400,512]{1,0:T(8,128)S(1)} %get-tuple-element.31, s32[512]{0:T(512)S(1)} %bitcast.32), kind=kOutput, calls=%fused_computation.45 | convolution fusion | flops 314894336 | bytes 2050048 | tf_op jit(solution)/shard_map/dot_general | solution.py:28
  57.6 0.0 all-reduce.2.cloned.1.call-update
  57.6 0.0 copy-start.5
  57.6 2.8 %divide_subtract_fusion.1 = f32[400,768]{1,0:T(8,128)} fusion(f32[400,768]{1,0:T(8,128)} %get-tuple-element.33, f32[768]{0:T(1024)S(1)} %get-tuple-element.10, f32[400,768]{1,0:T(8,128)S(1)} %copy-done, f32[768]{0:T(1024)S(1)} %sqrt_add_fusion.3, f32[400,768]{1,0:T(8,128)S(1)} %get-tuple-element.30), kind=kLoop, calls=%fused_computation.39 | loop fusion | flops 1843200 | bytes 4921344 | tf_op jit(solution)/shard_map/sub | solution.py:33
  60.3 0.0 copy-done.5
  60.3 0.0 copy-start.4
  60.4 2.4 %multiply_reduce_fusion = (f32[768]{0:T(1024)S(1)}, f32[400,768]{1,0:T(8,128)S(1)}) fusion(s32[1024]{0:T(1024)S(1)} %pad_add_fusion.1, f32[400,512]{1,0:T(8,128)S(1)} %copy-done.5, f32[400,512]{1,0:T(8,128)S(1)} %broadcast_multiply_fusion), kind=kOutput, calls=%fused_computation.38 | convolution fusion | flops 3776683264 | bytes 2874368 | tf_op jit(solution)/shard_map/dot_general | solution.py:28
  62.8 0.0 collective-permute-done.1
  62.8 0.6 sqrt_add_fusion
  63.4 0.0 copy-done.4
  63.4 0.0 copy-start.6
  63.4 1.2 %divide_subtract_fusion = f32[400,768]{1,0:T(8,128)} fusion(f32[400,768]{1,0:T(8,128)S(1)} %copy-done.4, f32[400,768]{1,0:T(8,128)S(1)} %get-tuple-element.35, f32[768]{0:T(1024)S(1)} %get-tuple-element.8), kind=kLoop, calls=%fused_computation.37 | loop fusion | flops 921600 | bytes 3689472 | tf_op jit(solution)/shard_map/sub | solution.py:33
  64.6 14.7 %all-reduce.2.cloned.1.call-done = f32[400,128]{1,0:T(8,128)} async-done(((f32[400,128]{1,0:T(8,128)}), f32[400,128]{1,0:T(8,128)}) %all-reduce.2.cloned.1.call-update) | async-done | bytes 204816 | tf_op jit(solution)/shard_map/psum | solution.py:102
  79.3 0.0 copy-done.6
  79.3 1.8 %divide_subtract_fusion.4 = (f32[400,128]{1,0:T(8,128)}, f32[400,128]{1,0:T(8,128)}) fusion(f32[400,128]{1,0:T(8,128)S(1)} %copy-done.1, f32[400,128]{1,0:T(8,128)} %all-reduce.2.cloned.1.call-done, f32[400,128]{1,0:T(8,128)S(1)} %copy-done.6), kind=kLoop, calls=%fused_computation.67 | loop fusion | flops 307200 | bytes 1024000 | tf_op jit(solution)/shard_map/sub | solution.py:104
  (6 shorter events, 0.1 us)
Async XLA Ops:
  7.2 72.1 %all-reduce.2.cloned.1.call-start = ((), (), s32[]{:S(2)}) async-start(), calls=%async_computation | async-start | bytes 409600 | tf_op jit(solution)/shard_map/psum | solution.py:102
  11.7 3.6 %copy-start = (f32[400,768]{1,0:T(8,128)S(1)}, f32[400,768]{1,0:T(8,128)}, u32[]{:S(2)}) copy-start(f32[400,768]{1,0:T(8,128)} %param.10) | copy-start | bytes 3686404
  20.4 2.5 %copy-start.8 = (f32[768]{0:T(1024)S(1)}, f32[768]{0:T(1024)}, u32[]{:S(2)}) copy-start(f32[768]{0:T(1024)} %param.13) | copy-start | bytes 9220
  20.4 3.0 %copy-start.2 = (f32[400,768]{1,0:T(8,128)S(1)}, f32[400,768]{1,0:T(8,128)}, u32[]{:S(2)}) copy-start(f32[400,768]{1,0:T(8,128)} %param.12) | copy-start | bytes 3686404
  22.9 39.9 %collective-permute-start.1 = (f32[768]{0:T(1024)S(1)}, f32[768]{0:T(1024)S(1)}, u32[]{:S(2)}, u32[]{:S(2)}) collective-permute-start(f32[768]{0:T(1024)S(1)} %get-tuple-element.15), channel_id=1, source_target_pairs={{0,2},{2,4},{4,6},{6,8},{8,10},{10,12},{12,14},{14,16},{16,18},{18... | collective-permute-start | bytes 9224 | tf_op jit(solution)/shard_map/ppermute | solution.py:14
  23.6 19.7 %collective-permute-start = (f32[400,768]{1,0:T(8,128)S(1)}, f32[400,768]{1,0:T(8,128)S(1)}, u32[]{:S(2)}, u32[]{:S(2)}) collective-permute-start(f32[400,768]{1,0:T(8,128)S(1)} %divide_subtract_fusion.2), channel_id=1, source_target_pairs={{0,2},{2,4},{4,6},{6,8},{8,10},{10,12},{12,14},{14,16},{16,18},{18... | collective-permute-start | bytes 3686408 | tf_op jit(solution)/shard_map/ppermute | solution.py:14
  28.0 1.4 %copy-start.7 = (f32[768]{0:T(1024)S(1)}, f32[768]{0:T(1024)}, u32[]{:S(2)}) copy-start(f32[768]{0:T(1024)} %param.11) | copy-start | bytes 9220
  28.0 1.4 %copy-start.1 = (f32[400,128]{1,0:T(8,128)S(1)}, f32[400,128]{1,0:T(8,128)}, u32[]{:S(2)}) copy-start(f32[400,128]{1,0:T(8,128)} %param.14) | copy-start | bytes 614404
  43.2 2.3 %copy-start.3 = (f32[400,768]{1,0:T(8,128)}, f32[400,768]{1,0:T(8,128)S(1)}, u32[]{:S(2)}) copy-start(f32[400,768]{1,0:T(8,128)S(1)} %collective-permute-done) | copy-start | bytes 3686404
  57.6 2.8 %copy-start.5 = (f32[400,512]{1,0:T(8,128)S(1)}, f32[400,512]{1,0:T(8,128)}, u32[]{:S(2)}) copy-start(f32[400,512]{1,0:T(8,128)} %fusion.55) | copy-start | bytes 2457604
  60.3 3.0 %copy-start.4 = (f32[400,768]{1,0:T(8,128)S(1)}, f32[400,768]{1,0:T(8,128)}, u32[]{:S(2)}) copy-start(f32[400,768]{1,0:T(8,128)} %copy-done.3) | copy-start | bytes 3686404
  63.4 15.9 %copy-start.6 = (f32[400,128]{1,0:T(8,128)S(1)}, f32[400,128]{1,0:T(8,128)}, u32[]{:S(2)}) copy-start(f32[400,128]{1,0:T(8,128)} %param.15) | copy-start | bytes 614404
Sparse Core Ops, SparseCore 0:
  57.7 21.5 all-reduce.1
where the time goes:
time: 88.3 us; the launch traced here: 87.9 us
  matrix products  32.3 us (37%)
  waiting for transfers between devices  27.5 us (31%)
  between operations  14.3 us (16%)
  other arithmetic  7.31 us (8%)
  starting transfers between devices  3.45 us (4%)
  local copies, waits for them, and re-layouts  3.11 us (4%)
    psum x1, waiting for transfers between devices, per_device(): summed = lax.psum(summed, 'rel')  14.7 us
    ppermute x2, waiting for transfers between devices, passed_along(): return lax.ppermute(value, axis, pairs)  12.8 us
    dot_general x6, matrix products, add_columns(): lax.dot_general(values, selector, (((1,), (1,)), ((), ())), precision=HIG...  10.6 us
    dot_general x6, matrix products, pick_columns(): return jnp.dot(matrix, selector, precision=HIGHEST)  10.6 us
    dot_general x2, matrix products, bucket_terms(): lax.dot_general(queries, negative, (((0,), (0,)), ((), ())), precision=HI...  4.18 us
    sub x3, other arithmetic, row_adagrad(): matrix - learn_rate * gradient / (jnp.sqrt(fresh) + epsilon)[None, :]  4.1 us
    dot_general x2, matrix products, bucket_terms(): grad_negative = jnp.dot(queries, neg_coef, precision=HIGHEST)  3.92 us
    ppermute x2, starting transfers between devices, passed_along(): return lax.ppermute(value, axis, pairs)  3.41 us
  transfers between devices with their start and end apart: 3, of which 2 were waited for; matrix products, arithmetic and copies ran while one was open for 29% of the time, Pallas kernels for 0%

commit v1 on v0

v1 whole, which is shorter than its diff:
```python
import functools

import jax
import jax.numpy as jnp
from jax import lax
from jax.experimental import pallas as pl
from jax.experimental.pallas import tpu as pltpu
from jax.sharding import PartitionSpec as P

learn_rate = 0.1
epsilon = 1e-06
MESH = pl.DeviceIdType.MESH
F32 = jnp.float32
BF16 = jnp.bfloat16


def split(x):
    high = x.astype(BF16)
    return high, (x - high.astype(F32)).astype(BF16)


def nn(a, b):
    return lax.dot_general(a, b, (((1,), (0,)), ((), ())), preferred_element_type=F32)


def nt(a, b):
    return lax.dot_general(a, b, (((1,), (1,)), ((), ())), preferred_element_type=F32)


def kernel(
    n_blk, n_rel, chunk,
    src_ref, srow_ref, tgt_ref, trow_ref, rel_ref, rstate_ref, sid_ref, rid_ref, tid_ref, nid_ref,
    out_src, out_srow, out_tgt, out_trow, out_rel, out_rstate,
    hot, rhot, table3, weight_hi, weight_lo, q3t, q_hi, q_lo, picked, relation, counts,
    send, recv, rel_all, send_sem, recv_sem, rsend_sem, rrecv_sem,
):
    dims, rows = src_ref.shape
    buckets, edges = sid_ref.shape
    negs = nid_ref.shape[1]
    rels = rel_ref.shape[1]
    chunks = rows // chunk
    pad = send.shape[2] - dims
    my_blk = lax.axis_index("blk")
    my_rel = lax.axis_index("rel")
    nxt = lax.rem(my_blk + 1, n_blk)
    prv = lax.rem(my_blk + n_blk - 1, n_blk)

    barrier = pltpu.get_barrier_semaphore()
    for other in (nxt, prv):
        pl.semaphore_signal(barrier, inc=1, device_id={"blk": other}, device_id_type=MESH)
    for step in range(1, n_rel):
        pl.semaphore_signal(
            barrier, inc=1, device_id={"rel": lax.rem(my_rel + step, n_rel)}, device_id_type=MESH
        )
    pl.semaphore_wait(barrier, 2 + n_rel - 1)

    def hop(bucket, c):
        return pltpu.make_async_remote_copy(
            src_ref=send.at[bucket, c],
            dst_ref=recv.at[bucket, c],
            send_sem=send_sem.at[bucket, c],
            recv_sem=recv_sem.at[bucket, c],
            device_id={"blk": nxt},
            device_id_type=MESH,
        )

    for bucket in range(buckets):
        last = bucket + 1 == buckets
        now_src = src_ref if bucket == 0 else out_src
        now_srow = srow_ref if bucket == 0 else out_srow
        sid = sid_ref[pl.ds(bucket, 1), :]
        rid = rid_ref[pl.ds(bucket, 1), :]
        hot[...] = (lax.broadcasted_iota(jnp.int32, (rows, edges), 0) == sid).astype(F32).astype(BF16)
        rhot[...] = (lax.broadcasted_iota(jnp.int32, (rels, edges), 0) == rid).astype(F32).astype(BF16)
        s_hi, s_lo = split(now_src[...])
        picked[...] = nn(s_hi, hot[...]) + nn(s_lo, hot[...])
        r_hi, r_lo = split(rel_ref[...])
        relation[...] = nn(r_hi, rhot[...]) + nn(r_lo, rhot[...])
        queries = picked[...] * relation[...]
        hi, lo = split(queries)
        q_hi[...] = hi
        q_lo[...] = lo
        hi_t = jnp.transpose(hi.astype(F32)).astype(BF16)
        lo_t = jnp.transpose(lo.astype(F32)).astype(BF16)
        q3t[0] = hi_t
        q3t[1] = lo_t
        tid = tid_ref[bucket]
        nid = nid_ref[bucket]

        for c in range(chunks):
            cols = pl.ds(c * chunk, chunk)
            lane = lax.broadcasted_iota(jnp.int32, (negs, chunk), 1) + c * chunk
            counts[:, cols] = jnp.sum(
                (lane == nid).astype(F32), axis=0, keepdims=True
            ) * (1.0 / negs)

        def do_chunk(c, carry):
            if bucket == 0:
                cols = pl.ds(pl.multiple_of(c * chunk, chunk), chunk)
                table = tgt_ref[:, cols]
                state = trow_ref[:, cols]
            else:
                cols = pl.ds(pl.multiple_of(c * chunk, chunk), chunk)
                hop(bucket - 1, c).wait_recv()
                table = recv[bucket - 1, c, :dims, :]
                state = recv[bucket - 1, c, dims:dims + 1, :]
            t_hi, t_lo = split(table)
            table3[0, c] = t_hi
            table3[1, c] = t_lo
            score = nn(q3t[0], t_hi) + nn(q3t[0], t_lo) + nn(q3t[1], t_hi)
            small = jnp.exp(-jnp.abs(score))
            large = 1.0 / (1.0 + small)
            small = small * large
            up = score >= 0
            sig = jnp.where(up, large, small)
            co = jnp.where(up, small, large)
            lane = lax.broadcasted_iota(jnp.int32, (edges, chunk), 1) + c * chunk
            weight = counts[:, cols] * sig - jnp.where(lane == tid, co, 0.0)
            w_hi, w_lo = split(weight)
            weight_hi[c] = w_hi
            weight_lo[c] = w_lo
            grad = nn(q_hi[...], w_hi) + nn(q_hi[...], w_lo) + nn(q_lo[...], w_hi)
            fresh = state + jnp.sum(grad * grad, axis=0, keepdims=True) * (1.0 / dims)
            new = table - grad * (learn_rate / (jnp.sqrt(fresh) + epsilon))
            if last:
                out_tgt[:, cols] = new
                out_trow[:, cols] = fresh
            else:
                send[bucket, c, :dims, :] = new
                send[bucket, c, dims:, :] = jnp.broadcast_to(fresh, (pad, chunk))
                hop(bucket, c).start()
            return carry

        lax.fori_loop(0, chunks, do_chunk, 0)

        grad_query = jnp.zeros((dims, edges), F32)
        for c in range(chunks):
            grad_query += (
                nt(table3[0, c], weight_hi[c])
                + nt(table3[0, c], weight_lo[c])
                + nt(table3[1, c], weight_hi[c])
            )
        g_hi, g_lo = split(grad_query * picked[...])
        rel_grad = nt(g_hi, rhot[...]) + nt(g_lo, rhot[...])
        if bucket == 0:
            rel_all[my_rel] = rel_grad
        else:
            rel_all[my_rel] = rel_all[my_rel] + rel_grad
        if last:
            for step in range(1, n_rel):
                peer = lax.rem(my_rel + step, n_rel)
                pltpu.make_async_remote_copy(
                    src_ref=rel_all.at[my_rel],
                    dst_ref=rel_all.at[my_rel],
                    send_sem=rsend_sem.at[step - 1],
                    recv_sem=rrecv_sem.at[my_rel],
                    device_id={"rel": peer},
                    device_id_type=MESH,
                ).start()
        g_hi, g_lo = split(grad_query * relation[...])
        src_grad = nt(g_hi, hot[...]) + nt(g_lo, hot[...])
        fresh = now_srow[...] + jnp.sum(src_grad * src_grad, axis=0, keepdims=True) * (1.0 / dims)
        out_src[...] = now_src[...] - src_grad * (learn_rate / (jnp.sqrt(fresh) + epsilon))
        out_srow[...] = fresh

    for bucket in range(buckets - 1):
        for c in range(chunks):
            hop(bucket, c).wait_send()
    for step in range(1, n_rel):
        peer = lax.rem(my_rel + n_rel - step, n_rel)
        arrived = pltpu.make_async_remote_copy(
            src_ref=rel_all.at[peer],
            dst_ref=rel_all.at[peer],
            send_sem=rsend_sem.at[step - 1],
            recv_sem=rrecv_sem.at[peer],
            device_id={"rel": peer},
            device_id_type=MESH,
        )
        arrived.wait_send()
        arrived.wait_recv()
    total = rel_all[0]
    for step in range(1, n_rel):
        total = total + rel_all[step]
    new_state = rstate_ref[...] + total * total
    out_rstate[...] = new_state
    out_rel[...] = rel_ref[...] - learn_rate * total / (jnp.sqrt(new_state) + epsilon)


def solution(mesh):
    n_blk, n_rel = mesh.shape["blk"], mesh.shape["rel"]

    def per_device(
        source_table, source_state, target_table, target_state, relation_ops, relation_state,
        source_ids, target_ids, relation_ids, negative_ids,
    ):
        dims, rows = source_table.shape
        rels = relation_ops.shape[1]
        buckets, edges = source_ids.shape
        chunk = 256 if rows % 256 == 0 else 128
        chunks = rows // chunk
        vmem = pl.BlockSpec(memory_space=pltpu.VMEM)
        shape = jax.ShapeDtypeStruct
        out = pl.pallas_call(
            functools.partial(kernel, n_blk, n_rel, chunk),
            out_shape=(
                shape((dims, rows), F32), shape((1, rows), F32),
                shape((dims, rows), F32), shape((1, rows), F32),
                shape((dims, rels), F32), shape((dims, rels), F32),
            ),
            in_specs=[vmem] * 10,
            out_specs=(vmem,) * 6,
            scratch_shapes=[
                pltpu.VMEM((rows, edges), BF16),
                pltpu.VMEM((rels, edges), BF16),
                pltpu.VMEM((2, chunks, dims, chunk), BF16),
                pltpu.VMEM((chunks, edges, chunk), BF16),
                pltpu.VMEM((chunks, edges, chunk), BF16),
                pltpu.VMEM((2, edges, dims), BF16),
                pltpu.VMEM((dims, edges), BF16),
                pltpu.VMEM((dims, edges), BF16),
                pltpu.VMEM((dims, edges), F32),
                pltpu.VMEM((dims, edges), F32),
                pltpu.VMEM((1, rows), F32),
                pltpu.VMEM((buckets - 1, chunks, dims + 8, chunk), F32),
                pltpu.VMEM((buckets - 1, chunks, dims + 8, chunk), F32),
                pltpu.VMEM((n_rel, dims, rels), F32),
                pltpu.SemaphoreType.DMA((buckets - 1, chunks)),
                pltpu.SemaphoreType.DMA((buckets - 1, chunks)),
                pltpu.SemaphoreType.DMA((n_rel,)),
                pltpu.SemaphoreType.DMA((n_rel,)),
            ],
            compiler_params=pltpu.CompilerParams(
                collective_id=0, has_side_effects=True, vmem_limit_bytes=60 * 1024 * 1024
            ),
        )(
            source_table, source_state[None, :], target_table, target_state[None, :],
            relation_ops, relation_state, source_ids, relation_ids,
            target_ids[:, :, None], negative_ids[:, :, None],
        )
        return (out[0], out[1][0], out[2], out[3][0], out[4], out[5])

    split_both = ("blk", "rel")
    return jax.shard_map(
        per_device,
        mesh=mesh,
        in_specs=(
            P(None, split_both), P(split_both), P(None, split_both), P(split_both),
            P(None, "blk"), P(None, "blk"),
            P(None, split_both), P(None, split_both), P(None, split_both), P(None, split_both),
        ),
        out_specs=(
            P(None, split_both), P(split_both), P(None, split_both), P(split_both),
            P(None, "blk"), P(None, "blk"),
        ),
        check_vma=False,
    )
```

time: 88.3 us -> 51.1 us (0.58)
  Pallas kernels: 0 us -> 36.6 us
  matrix products: 32.3 us -> 0 us
  waiting for transfers between devices: 27.5 us -> 0 us
  between operations: 14.3 us -> 0.65 us
  local copies, waits for them, and re-layouts: 3.11 us -> 10.9 us
  other arithmetic: 7.31 us -> 2.56 us
  starting transfers between devices: 3.45 us -> 0 us
    pallas_call x0 -> x1, Pallas kernels: none -> 36.6 us  [per_device(): pl.pallas_call(functools.partial(kernel, n_blk, n_rel, chunk), out_shape=...]
    dot_general x18 -> x0, matrix products: 32.3 us -> none  [the longest x6 10.6 us: add_columns(): lax.dot_general(values, selector, (((1,), (1,)), ((), ())), precision=HIG...]
    psum x1 -> x0, waiting for transfers between devices: 14.7 us -> none  [per_device(): summed = lax.psum(summed, 'rel')]
    ppermute x2 -> x0, waiting for transfers between devices: 12.8 us -> none  [passed_along(): return lax.ppermute(value, axis, pairs)]
    broadcast_in_dim x0 -> x4, local copies, waits for them, and re-layouts: none -> 5.94 us  [the longest x1 1.71 us: per_device(): target_ids[:, :, None]]
    sub x4 -> x0, other arithmetic: 5.87 us -> none  [the longest x3 4.1 us: row_adagrad(): matrix - learn_rate * gradient / (jnp.sqrt(fresh) + epsilon)[None, :]]
    unnamed x18 -> x10, local copies, waits for them, and re-layouts: 0.05 us -> 4.98 us
    ppermute x2 -> x0, starting transfers between devices: 3.41 us -> none  [passed_along(): return lax.ppermute(value, axis, pairs)]
  transfers between devices with their start and end apart: 3 -> 0, of which waited for: 2 -> 0; matrix products, arithmetic and copies ran while one was open for 29% -> 0% of each run, Pallas kernels for 0% -> 0%
where the time goes in v1:
time: 51.1 us; the launch traced here: 50.7 us
  Pallas kernels  36.6 us (72%)
  local copies, waits for them, and re-layouts  10.9 us (21%)
  other arithmetic  2.56 us (5%)
  between operations  0.65 us (1%)
    pallas_call x1, Pallas kernels, per_device(): pl.pallas_call(functools.partial(kernel, n_blk, n_rel, chunk), out_shape=...  36.6 us
    unnamed x10, local copies, waits for them, and re-layouts  4.98 us
    pallas_call x2, other arithmetic, per_device(): pl.pallas_call(functools.partial(kernel, n_blk, n_rel, chunk), out_shape=...  2.56 us
    broadcast_in_dim x1, local copies, waits for them, and re-layouts, per_device(): target_ids[:, :, None]  1.71 us
    broadcast_in_dim x1, local copies, waits for them, and re-layouts, per_device(): negative_ids[:, :, None]  1.71 us
    broadcast_in_dim x1, local copies, waits for them, and re-layouts, per_device(): source_state[None, :]  1.27 us
    broadcast_in_dim x1, local copies, waits for them, and re-layouts, per_device(): target_state[None, :]  1.27 us

profile of v1, /device:TPU:0, one launch (start us, length us, event | category | flops | bytes accessed | tf_op | source)
XLA Modules:
  0.0 50.7 jit_solution(13283090770325165348)
XLA Ops:
  0.6 1.7 %copy.16.tid_ref = s32[2,512,1]{2,1,0:T(8,128)} copy(s32[2,512,1]{1,0,2:T(2,128)} %bitcast.2) | data formatting | bytes 8192 | tf_op jit(solution)/shard_map/broadcast_in_dim | solution.py:238
  2.3 1.7 %copy.17.nid_ref = s32[2,512,1]{2,1,0:T(8,128)} copy(s32[2,512,1]{1,0,2:T(2,128)} %bitcast.3) | data formatting | bytes 8192 | tf_op jit(solution)/shard_map/broadcast_in_dim | solution.py:238
  4.0 1.3 %broadcast_in_dim.12.srow_ref = f32[1,768]{1,0:T(1,128)} reshape(f32[768]{0:T(1024)} %param.11) | data formatting | bytes 6144 | tf_op jit(solution)/shard_map/broadcast_in_dim | solution.py:236
  5.3 1.3 %broadcast_in_dim.13.trow_ref = f32[1,768]{1,0:T(1,128)} reshape(f32[768]{0:T(1024)} %param.13) | data formatting | bytes 6144 | tf_op jit(solution)/shard_map/broadcast_in_dim | solution.py:236
  6.6 36.6 %shard_map.145 = (f32[400,768]{1,0:T(8,128)}, f32[1,768]{1,0:T(1,128)}, f32[400,768]{1,0:T(8,128)}, f32[1,768]{1,0:T(1,128)}, f32[400,128]{1,0:T(8,128)}, /*index=5*/f32[400,128]{1,0:T(8,128)}) custom-call(f32[400,768]{1,0:T(8,128)} %src_ref.1, f32[1,768]{1,0:T(1,128)} %broadcast_in_dim.12.srow_ref, f32[400,768]{1,0:T(8,128)} %tgt_ref.1, ...), custom_call_target="tpu_custom_call" | custom-call | tf_op jit(solution)/shard_map/pallas_call | solution.py:203
  43.2 1.3 %reduce = f32[768]{0:T(1024)} reduce(f32[1,768]{1,0:T(1,128)} %get-tuple-element.13, f32[]{:T(128)} %constant), dimensions={0}, to_apply=%get-tuple-element.13.reduce_sub_computation | reduce | bytes 6148 | tf_op jit(solution)/shard_map/pallas_call | solution.py:203
  44.4 1.3 %reduce.1 = f32[768]{0:T(1024)} reduce(f32[1,768]{1,0:T(1,128)} %get-tuple-element.15, f32[]{:T(128)} %constant), dimensions={0}, to_apply=%get-tuple-element.15.reduce_sub_computation | reduce | bytes 6148 | tf_op jit(solution)/shard_map/pallas_call | solution.py:203
  45.7 0.0 copy-start
  45.7 2.5 %copy.22 = f32[400,768]{1,0:T(8,128)} copy(f32[400,768]{1,0:T(8,128)} %get-tuple-element.24) | data formatting | bytes 2457600
  48.2 0.0 copy-done
  48.2 0.0 copy-start.2
  48.2 0.0 copy-start.1
  48.2 1.0 %copy.23 = f32[400,768]{1,0:T(8,128)} copy(f32[400,768]{1,0:T(8,128)S(1)} %copy-done) | data formatting | bytes 2457600
  49.3 0.1 copy-done.2
  49.3 0.7 %copy.24 = f32[400,128]{1,0:T(8,128)} copy(f32[400,128]{1,0:T(8,128)S(1)} %copy-done.2) | data formatting | bytes 409600
  50.0 0.0 copy-done.1
  50.0 0.7 %copy.25 = f32[400,128]{1,0:T(8,128)} copy(f32[400,128]{1,0:T(8,128)S(1)} %copy-done.1) | data formatting | bytes 409600
Async XLA Ops:
  45.7 2.5 %copy-start = (f32[400,768]{1,0:T(8,128)S(1)}, f32[400,768]{1,0:T(8,128)}, u32[]{:S(2)}) copy-start(f32[400,768]{1,0:T(8,128)} %get-tuple-element.26) | copy-start | bytes 3686404
  48.2 1.1 %copy-start.2 = (f32[400,128]{1,0:T(8,128)S(1)}, f32[400,128]{1,0:T(8,128)}, u32[]{:S(2)}) copy-start(f32[400,128]{1,0:T(8,128)} %get-tuple-element.28) | copy-start | bytes 614404
  48.2 1.8 %copy-start.1 = (f32[400,128]{1,0:T(8,128)S(1)}, f32[400,128]{1,0:T(8,128)}, u32[]{:S(2)}) copy-start(f32[400,128]{1,0:T(8,128)} %get-tuple-element.29) | copy-start | bytes 614404

commit v2 on v1

--- a/solution.py
+++ b/solution.py
@@ -27,13 +27,39 @@
     return lax.dot_general(a, b, (((1,), (1,)), ((), ())), preferred_element_type=F32)
 
 
+def column(row):
+    wide = jnp.broadcast_to(row.astype(F32), (8, row.shape[1]))
+    return jnp.transpose(wide)[:, :1].astype(jnp.int32)
+
+
+def emit(*refs):
+    half = len(refs) // 2
+    inputs, outputs, sem = refs[:half], refs[half:-1], refs[-1]
+    copies = []
+    for i in (0, 2, 4, 5):
+        copies.append(pltpu.make_async_copy(inputs[i], outputs[i], sem.at[i]))
+        copies[-1].start()
+    for i in (1, 3):
+        outputs[i][...] = inputs[i][0, :]
+    for copy in copies:
+        copy.wait()
+
+
 def kernel(
     n_blk, n_rel, chunk,
+    src_in, srow_in, tgt_in, trow_in, rel_in, rstate_in, sid_in, rid_in, tid_in, nid_in,
+    out_src, out_srow, out_tgt, out_trow, out_rel, out_rstate,
     src_ref, srow_ref, tgt_ref, trow_ref, rel_ref, rstate_ref, sid_ref, rid_ref, tid_ref, nid_ref,
-    out_src, out_srow, out_tgt, out_trow, out_rel, out_rstate,
-    hot, rhot, table3, weight_hi, weight_lo, q3t, q_hi, q_lo, picked, relation, counts,
+    load_sem, hot, rhot, table3, weight_hi, weight_lo, q3t, q_hi, q_lo, picked, relation, gq_ref, counts,
     send, recv, rel_all, send_sem, recv_sem, rsend_sem, rrecv_sem,
 ):
+    loads = {}
+    for index, (there, here) in enumerate((
+        (sid_in, sid_ref), (rid_in, rid_ref), (rel_in, rel_ref), (src_in, src_ref), (tid_in, tid_ref),
+        (nid_in, nid_ref), (trow_in, trow_ref), (tgt_in, tgt_ref), (srow_in, srow_ref), (rstate_in, rstate_ref),
+    )):
+        loads[index] = pltpu.make_async_copy(there, here, load_sem.at[index])
+        loads[index].start()
     dims, rows = src_ref.shape
     buckets, edges = sid_ref.shape
     negs = nid_ref.shape[1]
@@ -52,7 +78,6 @@
         pl.semaphore_signal(
             barrier, inc=1, device_id={"rel": lax.rem(my_rel + step, n_rel)}, device_id_type=MESH
         )
-    pl.semaphore_wait(barrier, 2 + n_rel - 1)
 
     def hop(bucket, c):
         return pltpu.make_async_remote_copy(
@@ -64,10 +89,12 @@
             device_id_type=MESH,
         )
 
+    for index in range(4):
+        loads[index].wait()
+
     for bucket in range(buckets):
         last = bucket + 1 == buckets
         now_src = src_ref if bucket == 0 else out_src
-        now_srow = srow_ref if bucket == 0 else out_srow
         sid = sid_ref[pl.ds(bucket, 1), :]
         rid = rid_ref[pl.ds(bucket, 1), :]
         hot[...] = (lax.broadcasted_iota(jnp.int32, (rows, edges), 0) == sid).astype(F32).astype(BF16)
@@ -84,8 +111,11 @@
         lo_t = jnp.transpose(lo.astype(F32)).astype(BF16)
         q3t[0] = hi_t
         q3t[1] = lo_t
-        tid = tid_ref[bucket]
-        nid = nid_ref[bucket]
+        if bucket == 0:
+            for index in range(4, 10):
+                loads[index].wait()
+        tid = column(tid_ref[pl.ds(bucket, 1), :])
+        nid = column(nid_ref[pl.ds(bucket, 1), :])
 
         for c in range(chunks):
             cols = pl.ds(c * chunk, chunk)
@@ -94,19 +124,23 @@
                 (lane == nid).astype(F32), axis=0, keepdims=True
             ) * (1.0 / negs)
 
+        if bucket == 0:
+            pl.semaphore_wait(barrier, 2 + n_rel - 1)
+
         def do_chunk(c, carry):
             if bucket == 0:
                 cols = pl.ds(pl.multiple_of(c * chunk, chunk), chunk)
                 table = tgt_ref[:, cols]
-                state = trow_ref[:, cols]
+                state = trow_ref[cols].reshape(1, chunk)
             else:
                 cols = pl.ds(pl.multiple_of(c * chunk, chunk), chunk)
                 hop(bucket - 1, c).wait_recv()
                 table = recv[bucket - 1, c, :dims, :]
                 state = recv[bucket - 1, c, dims:dims + 1, :]
             t_hi, t_lo = split(table)
-            table3[0, c] = t_hi
-            table3[1, c] = t_lo
+            if bucket == 0:
+                table3[0, c] = t_hi
+                table3[1, c] = t_lo
             score = nn(q3t[0], t_hi) + nn(q3t[0], t_lo) + nn(q3t[1], t_hi)
             small = jnp.exp(-jnp.abs(score))
             large = 1.0 / (1.0 + small)
@@ -117,8 +151,11 @@
             lane = lax.broadcasted_iota(jnp.int32, (edges, chunk), 1) + c * chunk
             weight = counts[:, cols] * sig - jnp.where(lane == tid, co, 0.0)
             w_hi, w_lo = split(weight)
-            weight_hi[c] = w_hi
-            weight_lo[c] = w_lo
+            if bucket == 0:
+                weight_hi[c] = w_hi
+                weight_lo[c] = w_lo
+            else:
+                gq_ref[...] += nt(t_hi, w_hi) + nt(t_hi, w_lo) + nt(t_lo, w_hi)
             grad = nn(q_hi[...], w_hi) + nn(q_hi[...], w_lo) + nn(q_lo[...], w_hi)
             fresh = state + jnp.sum(grad * grad, axis=0, keepdims=True) * (1.0 / dims)
             new = table - grad * (learn_rate / (jnp.sqrt(fresh) + epsilon))
@@ -131,15 +168,20 @@
                 hop(bucket, c).start()
             return carry
 
+        if bucket > 0:
+            gq_ref[...] = jnp.zeros_like(gq_ref)
         lax.fori_loop(0, chunks, do_chunk, 0)
 
-        grad_query = jnp.zeros((dims, edges), F32)
-        for c in range(chunks):
-            grad_query += (
-                nt(table3[0, c], weight_hi[c])
-                + nt(table3[0, c], weight_lo[c])
-                + nt(table3[1, c], weight_hi[c])
-            )
+        if bucket == 0:
+            grad_query = jnp.zeros((dims, edges), F32)
+            for c in range(chunks):
+                grad_query += (
+                    nt(table3[0, c], weight_hi[c])
+                    + nt(table3[0, c], weight_lo[c])
+                    + nt(table3[1, c], weight_hi[c])
+                )
+        else:
+            grad_query = gq_ref[...]
         g_hi, g_lo = split(grad_query * picked[...])
         rel_grad = nt(g_hi, rhot[...]) + nt(g_lo, rhot[...])
         if bucket == 0:
@@ -159,7 +201,8 @@
                 ).start()
         g_hi, g_lo = split(grad_query * relation[...])
         src_grad = nt(g_hi, hot[...]) + nt(g_lo, hot[...])
-        fresh = now_srow[...] + jnp.sum(src_grad * src_grad, axis=0, keepdims=True) * (1.0 / dims)
+        now_srow = srow_ref[...].reshape(1, rows) if bucket == 0 else out_srow[...]
+        fresh = now_srow + jnp.sum(src_grad * src_grad, axis=0, keepdims=True) * (1.0 / dims)
         out_src[...] = now_src[...] - src_grad * (learn_rate / (jnp.sqrt(fresh) + epsilon))
         out_srow[...] = fresh
 
@@ -203,13 +246,18 @@
         out = pl.pallas_call(
             functools.partial(kernel, n_blk, n_rel, chunk),
             out_shape=(
-                shape((dims, rows), F32), shape((1, rows), F32),
-                shape((dims, rows), F32), shape((1, rows), F32),
-                shape((dims, rels), F32), shape((dims, rels), F32),
+                pltpu.VMEM((dims, rows), F32), pltpu.VMEM((1, rows), F32),
+                pltpu.VMEM((dims, rows), F32), pltpu.VMEM((1, rows), F32),
+                pltpu.VMEM((dims, rels), F32), pltpu.VMEM((dims, rels), F32),
             ),
-            in_specs=[vmem] * 10,
+            in_specs=[pl.BlockSpec(memory_space=pltpu.HBM)] * 10,
             out_specs=(vmem,) * 6,
             scratch_shapes=[
+                pltpu.VMEM((dims, rows), F32), pltpu.VMEM((rows,), F32),
+                pltpu.VMEM((dims, rows), F32), pltpu.VMEM((rows,), F32),
+                pltpu.VMEM((dims, rels), F32), pltpu.VMEM((dims, rels), F32),
+                *[pltpu.VMEM(ids.shape, jnp.int32) for ids in (source_ids, relation_ids, target_ids, negative_ids)],
+                pltpu.SemaphoreType.DMA((10,)),
                 pltpu.VMEM((rows, edges), BF16),
                 pltpu.VMEM((rels, edges), BF16),
                 pltpu.VMEM((2, chunks, dims, chunk), BF16),
@@ -218,6 +266,7 @@
                 pltpu.VMEM((2, edges, dims), BF16),
                 pltpu.VMEM((dims, edges), BF16),
                 pltpu.VMEM((dims, edges), BF16),
+                pltpu.VMEM((dims, edges), F32),
                 pltpu.VMEM((dims, edges), F32),
                 pltpu.VMEM((dims, edges), F32),
                 pltpu.VMEM((1, rows), F32),
@@ -230,14 +279,28 @@
                 pltpu.SemaphoreType.DMA((n_rel,)),
             ],
             compiler_params=pltpu.CompilerParams(
-                collective_id=0, has_side_effects=True, vmem_limit_bytes=60 * 1024 * 1024
+                collective_id=0, has_side_effects=True, vmem_limit_bytes=40 * 1024 * 1024
             ),
-        )(
-            source_table, source_state[None, :], target_table, target_state[None, :],
-            relation_ops, relation_state, source_ids, relation_ids,
-            target_ids[:, :, None], negative_ids[:, :, None],
-        )
-        return (out[0], out[1][0], out[2], out[3][0], out[4], out[5])
+        )(*(
+            pltpu.with_memory_space_constraint(x, pltpu.HBM) for x in (
+                source_table, source_state, target_table, target_state,
+                relation_ops, relation_state, source_ids, relation_ids,
+                target_ids, negative_ids,
+            )
+        ))
+        hbm = pl.BlockSpec(memory_space=pl.ANY)
+        return pl.pallas_call(
+            emit,
+            out_shape=(
+                shape((dims, rows), F32), shape((rows,), F32),
+                shape((dims, rows), F32), shape((rows,), F32),
+                shape((dims, rels), F32), shape((dims, rels), F32),
+            ),
+            in_specs=[vmem] * 6,
+            out_specs=(hbm, vmem, hbm, vmem, hbm, hbm),
+            scratch_shapes=[pltpu.SemaphoreType.DMA((6,))],
+            compiler_params=pltpu.CompilerParams(vmem_limit_bytes=16 * 1024 * 1024),
+        )(*out)
 
     split_both = ("blk", "rel")
     return jax.shard_map(

time: 51.1 us -> 36.6 us (0.72)
  local copies, waits for them, and re-layouts: 10.9 us -> 0 us
  other arithmetic: 2.56 us -> 0 us
  Pallas kernels: 36.6 us -> 35.8 us
    broadcast_in_dim x4 -> x0, local copies, waits for them, and re-layouts: 5.94 us -> none  [the longest x1 1.71 us: per_device(): target_ids[:, :, None]]
    unnamed x10 -> x0, local copies, waits for them, and re-layouts: 4.98 us -> none
    pallas_call x1, Pallas kernels: 36.6 us -> 33.6 us  [per_device(): pl.pallas_call(functools.partial(kernel, n_blk, n_rel, chunk), out_shape=...]
    pallas_call x2 -> x0, other arithmetic: 2.56 us -> none  [per_device(): pl.pallas_call(functools.partial(kernel, n_blk, n_rel, chunk), out_shape=...]
    pallas_call x0 -> x1, Pallas kernels: none -> 2.19 us  [per_device(): pl.pallas_call(emit, out_shape=(shape((dims, rows), F32), shape((rows,),...]
where the time goes in v2:
time: 36.6 us; the launch traced here: 36.4 us
  Pallas kernels  35.8 us (98%)
  between operations  0.64 us (2%)
    pallas_call x1, Pallas kernels, per_device(): pl.pallas_call(functools.partial(kernel, n_blk, n_rel, chunk), out_shape=...  33.6 us
    pallas_call x1, Pallas kernels, per_device(): pl.pallas_call(emit, out_shape=(shape((dims, rows), F32), shape((rows,),...  2.19 us

profile of v2, /device:TPU:0, one launch (start us, length us, event | category | flops | bytes accessed | tf_op | source)
XLA Modules:
  0.0 36.4 jit_solution(3191788608308651768)
XLA Ops:
  0.6 33.6 %shard_map.145 = (f32[400,768]{1,0:T(8,128)S(1)}, f32[1,768]{1,0:T(1,128)S(1)}, f32[400,768]{1,0:T(8,128)S(1)}, f32[1,768]{1,0:T(1,128)S(1)}, f32[400,128]{1,0:T(8,128)S(1)}, /*index=5*/f32[400,128]{1,0:T(8,128)S(1)}) custom-call(f32[400,768]{1,0:T(8,128)} %src_in.1, f32[768]{0:T(1024)} %srow_in.1, f32[400,768]{1,0:T(8,128)} %tgt_in.1, f32[768]{0:T(1024)} %trow_in.1, ...), custom_call_target="tpu_custom_call" | custom-call | tf_op jit(solution)/shard_map/pallas_call | solution.py:246
  34.2 2.2 %shard_map.146 = (f32[400,768]{1,0:T(8,128)}, f32[768]{0:T(1024)}, f32[400,768]{1,0:T(8,128)}, f32[768]{0:T(1024)}, f32[400,128]{1,0:T(8,128)}, /*index=5*/f32[400,128]{1,0:T(8,128)}) custom-call(f32[400,768]{1,0:T(8,128)S(1)} %get-tuple-element.12.refs_0_, f32[1,768]{1,0:T(1,128)S(1)} %get-tuple-element.13.refs_1_, ...), custom_call_target="tpu_custom_call" | custom-call | tf_op jit(solution)/shard_map/pallas_call | solution.py:292

commit v3 on v2

--- a/solution.py
+++ b/solution.py
@@ -33,14 +33,15 @@
 
 
 def emit(*refs):
-    half = len(refs) // 2
-    inputs, outputs, sem = refs[:half], refs[half:-1], refs[-1]
+    inputs, outputs, (first, second, sem) = refs[:6], refs[6:12], refs[12:]
     copies = []
     for i in (0, 2, 4, 5):
         copies.append(pltpu.make_async_copy(inputs[i], outputs[i], sem.at[i]))
         copies[-1].start()
-    for i in (1, 3):
-        outputs[i][...] = inputs[i][0, :]
+    for i, line in ((1, first), (3, second)):
+        line[...] = inputs[i][0, :]
+        copies.append(pltpu.make_async_copy(line, outputs[i], sem.at[i]))
+        copies[-1].start()
     for copy in copies:
         copy.wait()
 
@@ -127,16 +128,13 @@
         if bucket == 0:
             pl.semaphore_wait(barrier, 2 + n_rel - 1)
 
-        def do_chunk(c, carry):
+        def weigh(c):
+            cols = pl.ds(pl.multiple_of(c * chunk, chunk), chunk)
             if bucket == 0:
-                cols = pl.ds(pl.multiple_of(c * chunk, chunk), chunk)
                 table = tgt_ref[:, cols]
-                state = trow_ref[cols].reshape(1, chunk)
             else:
-                cols = pl.ds(pl.multiple_of(c * chunk, chunk), chunk)
                 hop(bucket - 1, c).wait_recv()
                 table = recv[bucket - 1, c, :dims, :]
-                state = recv[bucket - 1, c, dims:dims + 1, :]
             t_hi, t_lo = split(table)
             if bucket == 0:
                 table3[0, c] = t_hi
@@ -151,11 +149,22 @@
             lane = lax.broadcasted_iota(jnp.int32, (edges, chunk), 1) + c * chunk
             weight = counts[:, cols] * sig - jnp.where(lane == tid, co, 0.0)
             w_hi, w_lo = split(weight)
+            weight_hi[c] = w_hi
+            weight_lo[c] = w_lo
+            if bucket > 0:
+                part = nt(t_hi, w_hi) + nt(t_hi, w_lo) + nt(t_lo, w_hi)
+                gq_ref[...] = part if isinstance(c, int) and c == 0 else gq_ref[...] + part
+
+        def finish(c):
+            cols = pl.ds(pl.multiple_of(c * chunk, chunk), chunk)
             if bucket == 0:
-                weight_hi[c] = w_hi
-                weight_lo[c] = w_lo
+                table = tgt_ref[:, cols]
+                state = trow_ref[cols].reshape(1, chunk)
             else:
-                gq_ref[...] += nt(t_hi, w_hi) + nt(t_hi, w_lo) + nt(t_lo, w_hi)
+                table = recv[bucket - 1, c, :dims, :]
+                state = recv[bucket - 1, c, dims:dims + 1, :]
+            w_hi = weight_hi[c]
+            w_lo = weight_lo[c]
             grad = nn(q_hi[...], w_hi) + nn(q_hi[...], w_lo) + nn(q_lo[...], w_hi)
             fresh = state + jnp.sum(grad * grad, axis=0, keepdims=True) * (1.0 / dims)
             new = table - grad * (learn_rate / (jnp.sqrt(fresh) + epsilon))
@@ -166,12 +175,20 @@
                 send[bucket, c, :dims, :] = new
                 send[bucket, c, dims:, :] = jnp.broadcast_to(fresh, (pad, chunk))
                 hop(bucket, c).start()
-            return carry
-
-        if bucket > 0:
-            gq_ref[...] = jnp.zeros_like(gq_ref)
-        lax.fori_loop(0, chunks, do_chunk, 0)
-
+
+        if bucket == 0:
+
+            def both(c, carry):
+                weigh(c)
+                finish(c)
+                return carry
+
+            lax.fori_loop(0, chunks, both, 0)
+        else:
+            for c in range(chunks):
+                weigh(c)
+                if not last or c + 1 < chunks:
+                    finish(c)
         if bucket == 0:
             grad_query = jnp.zeros((dims, edges), F32)
             for c in range(chunks):
@@ -199,6 +216,8 @@
                     device_id={"rel": peer},
                     device_id_type=MESH,
                 ).start()
+        if last and bucket > 0:
+            finish(chunks - 1)
         g_hi, g_lo = split(grad_query * relation[...])
         src_grad = nt(g_hi, hot[...]) + nt(g_lo, hot[...])
         now_srow = srow_ref[...].reshape(1, rows) if bucket == 0 else out_srow[...]
@@ -297,8 +316,8 @@
                 shape((dims, rels), F32), shape((dims, rels), F32),
             ),
             in_specs=[vmem] * 6,
-            out_specs=(hbm, vmem, hbm, vmem, hbm, hbm),
-            scratch_shapes=[pltpu.SemaphoreType.DMA((6,))],
+            out_specs=(hbm,) * 6,
+            scratch_shapes=[pltpu.VMEM((rows,), F32), pltpu.VMEM((rows,), F32), pltpu.SemaphoreType.DMA((6,))],
             compiler_params=pltpu.CompilerParams(vmem_limit_bytes=16 * 1024 * 1024),
         )(*out)
 

time: 36.6 us -> 35.5 us (0.970)
  Pallas kernels: 35.8 us -> 34.6 us
    pallas_call x1, Pallas kernels: 33.6 us -> 33 us  [per_device(): pl.pallas_call(functools.partial(kernel, n_blk, n_rel, chunk), out_shape=...]
    pallas_call x1, Pallas kernels: 2.19 us -> 1.62 us  [per_device(): pl.pallas_call(emit, out_shape=(shape((dims, rows), F32), shape((rows,),...]
where the time goes in v3:
time: 35.5 us; the launch traced here: 35.3 us
  Pallas kernels  34.6 us (97%)
  between operations  0.64 us (2%)
    pallas_call x1, Pallas kernels, per_device(): pl.pallas_call(functools.partial(kernel, n_blk, n_rel, chunk), out_shape=...  33 us
    pallas_call x1, Pallas kernels, per_device(): pl.pallas_call(emit, out_shape=(shape((dims, rows), F32), shape((rows,),...  1.62 us

profile of v3, /device:TPU:0, one launch (start us, length us, event | category | flops | bytes accessed | tf_op | source)
XLA Modules:
  0.0 35.3 jit_solution(14266873187210159415)
XLA Ops:
  0.6 33.0 %shard_map.145 = (f32[400,768]{1,0:T(8,128)S(1)}, f32[1,768]{1,0:T(1,128)S(1)}, f32[400,768]{1,0:T(8,128)S(1)}, f32[1,768]{1,0:T(1,128)S(1)}, f32[400,128]{1,0:T(8,128)S(1)}, /*index=5*/f32[400,128]{1,0:T(8,128)S(1)}) custom-call(f32[400,768]{1,0:T(8,128)} %src_in.1, f32[768]{0:T(1024)} %srow_in.1, f32[400,768]{1,0:T(8,128)} %tgt_in.1, f32[768]{0:T(1024)} %trow_in.1, ...), custom_call_target="tpu_custom_call" | custom-call | tf_op jit(solution)/shard_map/pallas_call | solution.py:265
  33.7 1.6 %shard_map.146 = (f32[400,768]{1,0:T(8,128)}, f32[768]{0:T(1024)}, f32[400,768]{1,0:T(8,128)}, f32[768]{0:T(1024)}, f32[400,128]{1,0:T(8,128)}, /*index=5*/f32[400,128]{1,0:T(8,128)}) custom-call(f32[400,768]{1,0:T(8,128)S(1)} %get-tuple-element.12.refs_0_, f32[1,768]{1,0:T(1,128)S(1)} %get-tuple-element.13.refs_1_, ...), custom_call_target="tpu_custom_call" | custom-call | tf_op jit(solution)/shard_map/pallas_call | solution.py:311

commit v4 on v3

--- a/solution.py
+++ b/solution.py
@@ -56,8 +56,8 @@
 ):
     loads = {}
     for index, (there, here) in enumerate((
-        (sid_in, sid_ref), (rid_in, rid_ref), (rel_in, rel_ref), (src_in, src_ref), (tid_in, tid_ref),
-        (nid_in, nid_ref), (trow_in, trow_ref), (tgt_in, tgt_ref), (srow_in, srow_ref), (rstate_in, rstate_ref),
+        (sid_in, sid_ref), (rid_in, rid_ref), (tid_in, tid_ref), (nid_in, nid_ref), (rel_in, rel_ref),
+        (src_in, src_ref), (trow_in, trow_ref), (tgt_in, tgt_ref), (srow_in, srow_ref), (rstate_in, rstate_ref),
     )):
         loads[index] = pltpu.make_async_copy(there, here, load_sem.at[index])
         loads[index].start()
@@ -100,6 +100,19 @@
         rid = rid_ref[pl.ds(bucket, 1), :]
         hot[...] = (lax.broadcasted_iota(jnp.int32, (rows, edges), 0) == sid).astype(F32).astype(BF16)
         rhot[...] = (lax.broadcasted_iota(jnp.int32, (rels, edges), 0) == rid).astype(F32).astype(BF16)
+        tid = column(tid_ref[pl.ds(bucket, 1), :])
+        nid = column(nid_ref[pl.ds(bucket, 1), :])
+
+        for c in range(chunks):
+            cols = pl.ds(c * chunk, chunk)
+            lane = lax.broadcasted_iota(jnp.int32, (negs, chunk), 1) + c * chunk
+            counts[:, cols] = jnp.sum(
+                (lane == nid).astype(F32), axis=0, keepdims=True
+            ) * (1.0 / negs)
+
+        if bucket == 0:
+            for index in range(4, 6):
+                loads[index].wait()
         s_hi, s_lo = split(now_src[...])
         picked[...] = nn(s_hi, hot[...]) + nn(s_lo, hot[...])
         r_hi, r_lo = split(rel_ref[...])
@@ -113,18 +126,8 @@
         q3t[0] = hi_t
         q3t[1] = lo_t
         if bucket == 0:
-            for index in range(4, 10):
+            for index in range(6, 10):
                 loads[index].wait()
-        tid = column(tid_ref[pl.ds(bucket, 1), :])
-        nid = column(nid_ref[pl.ds(bucket, 1), :])
-
-        for c in range(chunks):
-            cols = pl.ds(c * chunk, chunk)
-            lane = lax.broadcasted_iota(jnp.int32, (negs, chunk), 1) + c * chunk
-            counts[:, cols] = jnp.sum(
-                (lane == nid).astype(F32), axis=0, keepdims=True
-            ) * (1.0 / negs)
-
         if bucket == 0:
             pl.semaphore_wait(barrier, 2 + n_rel - 1)
 

time: 35.5 us -> 35 us (0.986)
  Pallas kernels: 34.6 us -> 34.2 us
    pallas_call x1, Pallas kernels: 33 us -> 32.6 us  [per_device(): pl.pallas_call(functools.partial(kernel, n_blk, n_rel, chunk), out_shape=...]
where the time goes in v4:
time: 35 us; the launch traced here: 34.8 us
  Pallas kernels  34.2 us (98%)
  between operations  0.64 us (2%)
    pallas_call x1, Pallas kernels, per_device(): pl.pallas_call(functools.partial(kernel, n_blk, n_rel, chunk), out_shape=...  32.6 us
    pallas_call x1, Pallas kernels, per_device(): pl.pallas_call(emit, out_shape=(shape((dims, rows), F32), shape((rows,),...  1.62 us

profile of v4, /device:TPU:0, one launch (start us, length us, event | category | flops | bytes accessed | tf_op | source)
XLA Modules:
  0.0 34.8 jit_solution(3931871178875734308)
XLA Ops:
  0.6 32.6 %shard_map.145 = (f32[400,768]{1,0:T(8,128)S(1)}, f32[1,768]{1,0:T(1,128)S(1)}, f32[400,768]{1,0:T(8,128)S(1)}, f32[1,768]{1,0:T(1,128)S(1)}, f32[400,128]{1,0:T(8,128)S(1)}, /*index=5*/f32[400,128]{1,0:T(8,128)S(1)}) custom-call(f32[400,768]{1,0:T(8,128)} %src_in.1, f32[768]{0:T(1024)} %srow_in.1, f32[400,768]{1,0:T(8,128)} %tgt_in.1, f32[768]{0:T(1024)} %trow_in.1, ...), custom_call_target="tpu_custom_call" | custom-call | tf_op jit(solution)/shard_map/pallas_call | solution.py:268
  33.2 1.6 %shard_map.146 = (f32[400,768]{1,0:T(8,128)}, f32[768]{0:T(1024)}, f32[400,768]{1,0:T(8,128)}, f32[768]{0:T(1024)}, f32[400,128]{1,0:T(8,128)}, /*index=5*/f32[400,128]{1,0:T(8,128)}) custom-call(f32[400,768]{1,0:T(8,128)S(1)} %get-tuple-element.12.refs_0_, f32[1,768]{1,0:T(1,128)S(1)} %get-tuple-element.13.refs_1_, ...), custom_call_target="tpu_custom_call" | custom-call | tf_op jit(solution)/shard_map/pallas_call | solution.py:314
